TPU v7x, 32 devices: a whole 2x2x4 slice. The times are simulated.
32 devices in a mesh: dp: 4 (over y, x), vocab: 8 (over z, core).
Axes of the slice: x: 2, y: 2, z: 4, core: 2. Of those that a mesh axis runs over, the one named last changes fastest.
Arguments:
- hidden: bfloat16 [4, 32, 3584], P('dp', None, 'vocab'), may hold values from -6 to 6
- kl_hidden: bfloat16 [4, 32, 3584], P('dp', None, 'vocab'), may hold values from -6 to 6
- head_weight: bfloat16 [256000, 3584], P(('dp', 'vocab')), may hold values from -0.3125 to 0.3125
- labels: int32 [4, 32], P('dp'), may hold values from 0 to 255999
- token_mask: int32 [4, 32], P('dp'), may hold values 0 or 1
- kl_pair: int32 [4], P('dp'), may hold values from 0 to 3, as said below
- desirable: int32 [4], P('dp'), may hold values 0 or 1
- ref_logps: float32 [4, 64], P('dp', 'vocab'), may hold values from -23 to -11
Outputs:
- token_logps: float32 [4, 64], P('dp', 'vocab')
- seq_losses: float32 [4], P('dp')
- loss: float32 [], replicated
Inputs may be any that keep to these rules, and one draw needn't show every extreme that they name: kl_pair is a permutation of the 4 sequences with kl_pair[s] != s.
All inputs are finite; a program needn't handle non-finite values. No bound on the sum of `token_mask` or of `desirable` on one device may be relied on, other than what follows from the above.
Results may differ from a plain program's by a relative error of at most 0.0003.
Values may be sent and summed in bfloat16 or wider, within the bound.
A program may use at most 128 MiB of HBM per device.

v0:
```python
import jax
import jax.numpy as jnp
from jax import lax
from jax.sharding import PartitionSpec as P

kto_beta = 0.1
desirable_weight = 1.0
undesirable_weight = 1.33


def label_terms(logits, targets, first_row):
    shifted = targets - first_row
    inside = (shifted >= 0) & (shifted < logits.shape[1])
    clipped = jnp.clip(shifted, 0, logits.shape[1] - 1)
    picked = jnp.take_along_axis(logits, clipped[:, None], axis=1)[:, 0]
    return (jnp.sum(jnp.exp(logits), axis=1), jnp.where(inside, picked, 0.0))


def kto_losses(logratio, kl_total, seq_total, desirable):
    kl_estimate = kl_total / seq_total
    wanted = desirable_weight * (1.0 - jax.nn.sigmoid(kto_beta * (logratio - kl_estimate)))
    unwanted = undesirable_weight * (1.0 - jax.nn.sigmoid(kto_beta * (kl_estimate - logratio)))
    return jnp.where(desirable == 1, wanted, unwanted)


def on_device(hidden, kl_hidden, head_weight, labels, token_mask, kl_pair, desirable, ref_logps):
    sub_seq = hidden.shape[0]
    length = hidden.shape[1]
    vocab_rows = head_weight.shape[0]
    model_width = head_weight.shape[1]
    groups = lax.axis_size("vocab")
    vocab_index = lax.axis_index("vocab")
    data_index = lax.axis_index("dp")
    first_row = (data_index * groups + vocab_index) * vocab_rows
    all_labels, all_masks, all_pairs, all_desirable = (
        lax.all_gather(labels, "dp", axis=0, tiled=True),
        lax.all_gather(token_mask, "dp", axis=0, tiled=True),
        lax.all_gather(kl_pair, "dp", axis=0, tiled=True),
        lax.all_gather(desirable, "dp", axis=0, tiled=True),
    )
    targets = jnp.concatenate([all_labels, all_labels[all_pairs]], axis=1)
    weights_mask = jnp.concatenate([all_masks, all_masks[all_pairs]], axis=1).astype(jnp.float32)
    seq_total = targets.shape[0]
    columns = targets.shape[1]
    combined = jnp.concatenate([hidden, kl_hidden], axis=1)
    whole_rows = lax.all_gather(combined, "vocab", axis=2, tiled=True)
    portion = lax.all_gather(whole_rows, "dp", axis=0, tiled=True)
    number = portion.shape[0]
    logits = lax.dot_general(
        portion.reshape(number * columns, model_width),
        head_weight,
        (((1,), (1,)), ((), ())),
        preferred_element_type=jnp.float32,
    )
    portion_targets = targets.reshape(-1)
    part_sum, part_pick = label_terms(logits, portion_targets, first_row)
    token_stats = jnp.stack(
        [part_sum.reshape(number, columns), part_pick.reshape(number, columns)], axis=1
    )
    partition = token_stats[:, 0]
    picked = token_stats[:, 1]
    own_cols = columns // groups
    row_start = data_index * sub_seq
    col_start = vocab_index * own_cols
    ref_full = lax.dynamic_update_slice(
        jnp.zeros((seq_total, columns), jnp.float32), ref_logps, (row_start, col_start)
    )
    partition, picked, ref_all = lax.psum((partition, picked, ref_full), ("dp", "vocab"))
    token_logps = picked - jnp.log(partition)
    differences = weights_mask * (token_logps - ref_all)
    logratio = jnp.sum(differences[:, :length], axis=1)
    kl_terms = jnp.sum(differences[:, length:], axis=1)
    losses = kto_losses(logratio, jnp.sum(kl_terms), seq_total, all_desirable)
    own_logps = lax.dynamic_slice(token_logps, (row_start, col_start), (sub_seq, own_cols))
    own_losses = lax.dynamic_slice_in_dim(losses, row_start, sub_seq, 0)
    return (own_logps, own_losses, jnp.mean(losses))


def solution(mesh):
    in_specs = (
        P("dp", None, "vocab"),
        P("dp", None, "vocab"),
        P(("dp", "vocab"), None),
        P("dp", None),
        P("dp", None),
        P("dp"),
        P("dp"),
        P("dp", "vocab"),
    )
    out_specs = (P("dp", "vocab"), P("dp"), P())
    return jax.shard_map(
        on_device, mesh=mesh, in_specs=in_specs, out_specs=out_specs, check_vma=False
    )
```

profile of v0, /device:TPU:0, one launch (start us, length us, event | category | flops | bytes accessed | tf_op | source)
XLA Modules:
  0.0 153.5 jit_solution(2589287121122592298)
XLA Ops:
  7.2 0.8 pad_maximum_fusion
  8.0 0.2 copy.14
  8.2 23.7 %all_gather.20 = bf16[1,64,3584]{1,0,2:T(2,128)(2,1)S(1)} all-gather(bf16[1,64,448]{1,0,2:T(2,128)(2,1)S(1)} %copy.14), channel_id=1, replica_groups=mesh['dp'=4,'vocab'=8] {'vocab'}, dimensions={2}, use_global_device_ids=true | all-gather | bytes 516096 | tf_op jit(solution)/shard_map/all_gather | solution.py:46
  31.8 3.1 %copy.15 = bf16[1,64,3584]{2,1,0:T(8,128)(2,1)} copy(bf16[1,64,3584]{1,0,2:T(2,128)(2,1)S(1)} %all_gather.20) | data formatting | bytes 917504 | tf_op jit(solution)/shard_map/all_gather | solution.py:46
  36.2 1.2 dynamic-slice
  37.5 0.8 dynamic-update-slice
  38.3 0.8 dynamic-update-slice.1
  39.0 7.4 %all-reduce.2 = (s32[4]{0:T(128)S(1)}, s32[4]{0:T(128)S(1)}) all-reduce(s32[4]{0:T(128)S(1)} %dynamic-update-slice, s32[4]{0:T(128)S(1)} %dynamic-update-slice.1), channel_id=1, replica_groups=mesh['dp'=4,'vocab'=8] {'dp'}, use_global_device_ids=true, to_apply=%add | all-reduce | flops 8 | bytes 64
  46.4 7.9 %all-gather.1 = s32[4,1,32]{2,1,0:T(1,128)S(1)} all-gather(s32[1,1,32]{2,1,0:T(1,128)} %bitcast.17), channel_id=1, replica_groups=mesh['dp'=4,'vocab'=8] {'dp'}, dimensions={0}, use_global_device_ids=true | all-gather | bytes 640 | tf_op jit(solution)/shard_map/all_gather | solution.py:37
  54.3 0.6 gather_fusion.1
  54.9 7.2 %all-gather = s32[4,1,32]{2,1,0:T(1,128)S(1)} all-gather(s32[1,1,32]{2,1,0:T(1,128)} %bitcast.18), channel_id=1, replica_groups=mesh['dp'=4,'vocab'=8] {'dp'}, dimensions={0}, use_global_device_ids=true | all-gather | bytes 640 | tf_op jit(solution)/shard_map/all_gather | solution.py:36
  62.1 0.6 gather_fusion
  62.8 0.1 min.12
  62.8 0.8 dynamic_update_slice.3
  63.7 4.1 %all-gather.4.cloned.1.call-done = bf16[4,64,3584]{2,1,0:T(8,128)(2,1)} async-done(((bf16[1,64,3584]{2,1,0:T(8,128)(2,1)}), bf16[4,64,3584]{2,1,0:T(8,128)(2,1)}) %all-gather.4.cloned.1.call-update) | async-done | bytes 1835024 | tf_op jit(solution)/shard_map/all_gather | solution.py:47
  67.7 25.9 %exponential_reduce_fusion = (f32[256]{0:T(256)S(1)}, f32[256,8000]{0,1:T(8,128)}) fusion(bf16[256,3584]{1,0:T(8,128)(2,1)} %bitcast.19, bf16[8000,3584]{1,0:T(8,128)(2,1)} %param.10), kind=kOutput, calls=%fused_computation.3 | convolution fusion | flops 14682112000 | bytes 67372032 | tf_op jit(solution)/shard_map/dot_general | solution.py:49
  93.6 9.2 %gather_fusion.2 = f32[256]{0:T(256)S(1)} fusion(f32[256,8000]{0,1:T(8,128)} %get-tuple-element.15, s32[256]{0:T(256)S(1)} %bitcast.11), kind=kCustom, calls=%fused_computation.2 | custom fusion | bytes 4096 | tf_op jit(solution)/shard_map/jit(take_along_axis)/gather | solution.py:15
  102.8 0.1 gather.14
  102.9 0.1 select_select_fusion
  103.0 38.7 %all-reduce.3 = (f32[4,64]{1,0:T(4,128)S(1)}, f32[4,64]{1,0:T(4,128)S(1)}, f32[4,64]{1,0:T(4,128)S(1)}) all-reduce(f32[4,64]{1,0:T(4,128)S(1)} %select_select_fusion, f32[4,64]{1,0:T(4,128)S(1)} %squeeze_stack_reshape.4, f32[4,64]{1,0:T(4,128)S(1)} %dynamic_update_slice.3), channel_id=1, replica_groups=mesh['dp'=4,'vocab'=8] {'dp','vocab'}, use_global_device_ids=true, to_apply=%region_0.1 | all-reduce | flops 768 | bytes 6144 | tf_op jit(solution)/shard_map/psum | solution.py:68
  141.8 0.6 dynamic_slice.6
  142.3 0.7 slice_reduce_fusion
  143.7 0.6 fusion.4
  144.3 0.6 dynamic_slice.7
  (14 shorter events, 0.3 us)
Async XLA Ops:
  7.2 60.6 %all-gather.4.cloned.1.call-start = ((), (), s32[]{:S(2)}) async-start(), calls=%async_computation | async-start | bytes 2293760 | tf_op jit(solution)/shard_map/all_gather | solution.py:47
Sparse Core Ops, SparseCore 0:
  35.1 32.6 all-gather.3
where the time goes:
time: 154 us; the launch traced here: 153 us
  blocking collectives  84.9 us (55%)
  matrix products  25.9 us (17%)
  local copies, waits for them, and re-layouts  18.5 us (12%)
  between operations  17.8 us (12%)
  waiting for transfers between devices  4.07 us (3%)
  other arithmetic  2.34 us (2%)
    psum x1, blocking collectives, on_device(): lax.psum((partition, picked, ref_full), ('dp', 'vocab'))  38.7 us
    dot_general x1, matrix products, on_device(): lax.dot_general(portion.reshape(number * columns, model_width), head_weig...  25.9 us
    all_gather x1, blocking collectives, on_device(): whole_rows = lax.all_gather(combined, 'vocab', axis=2, tiled=True)  23.7 us
    gather x2, local copies, waits for them, and re-layouts, label_terms(): picked = jnp.take_along_axis(logits, clipped[:, None], axis=1)[:, 0]  9.27 us
    all_gather x1, blocking collectives, on_device(): lax.all_gather(token_mask, 'dp', axis=0, tiled=True)  7.92 us
    unnamed x1, blocking collectives  7.39 us
    all_gather x1, blocking collectives, on_device(): lax.all_gather(labels, 'dp', axis=0, tiled=True)  7.23 us
    all_gather x1, waiting for transfers between devices, on_device(): portion = lax.all_gather(whole_rows, 'dp', axis=0, tiled=True)  4.05 us
  transfers between devices with their start and end apart: 1, of which 1 were waited for; matrix products, arithmetic and copies ran while one was open for 3% of the time, Pallas kernels for 0%

commit v1 on v0

--- a/solution.py
+++ b/solution.py
@@ -1,7 +1,16 @@
+import functools
+
 import jax
 import jax.numpy as jnp
 from jax import lax
+from jax.experimental import pallas as pl
+from jax.experimental.pallas import tpu as pltpu
 from jax.sharding import PartitionSpec as P
+
+MESH = pl.DeviceIdType.MESH
+LANES = 128
+TILE_ROWS = 2000
+
 
 kto_beta = 0.1
 desirable_weight = 1.0
@@ -23,7 +32,7 @@
     return jnp.where(desirable == 1, wanted, unwanted)
 
 
-def on_device(hidden, kl_hidden, head_weight, labels, token_mask, kl_pair, desirable, ref_logps):
+def gathered_by_xla(hidden, kl_hidden, head_weight, labels, token_mask, kl_pair, desirable, ref_logps):
     sub_seq = hidden.shape[0]
     length = hidden.shape[1]
     vocab_rows = head_weight.shape[0]
@@ -76,6 +85,381 @@
     return (own_logps, own_losses, jnp.mean(losses))
 
 
+def fused_kernel(dims, hid, klh, weight, labels, mask, pair, flag, ref, out, held, wbuf, acc, xeven, xodd,
+                 lab_v, mask_v, pair_v, flag_v, ref_v, meta, sums, picks, red, xs, ms, ws, ici, d2d,
+                 s_plane, s_part, s_right, s_left, m_send, m_recv, r_send, r_recv):
+    seqs, groups = dims
+    depth = groups // 2
+    devices = seqs * groups
+    length = hid.shape[1]
+    columns = 2 * length
+    width = hid.shape[2]
+    chunk = 2 * width
+    vocab_rows = weight.shape[0]
+    tile = TILE_ROWS
+    tiles = vocab_rows // tile
+    positions = seqs * columns
+    d = lax.axis_index("dp")
+    v = lax.axis_index("vocab")
+    z = lax.div(v, 2)
+    c = lax.rem(v, 2)
+    me = d * groups + v
+    partner = (d, z * 2 + (1 - c))
+    above = (d, jnp.minimum(v + 2, groups - 1))
+    below = (d, jnp.maximum(v - 2, 0))
+    has_above = z + 1 < depth
+    has_below = z >= 1
+
+    def order(step):
+        least = jnp.minimum(z, depth - 1 - z)
+        near = (step + 1) // 2
+        inner = z - near if step % 2 else z + near
+        outer = jnp.where(z > depth - 1 - z, z - (step - least), z + (step - least))
+        return jnp.where(step <= 2 * least, inner, outer)
+
+    chunks = [order(step) for step in range(depth)]
+
+    def block(parity, zc, dc):
+        return held.at[parity, zc, pl.ds(pl.multiple_of(dc * columns, columns), columns)]
+
+    def weight_copies(p, i):
+        rows = pl.ds(pl.multiple_of(i * tile, tile), tile)
+        base = pl.multiple_of(chunks[p] * chunk, LANES)
+        if p % 2 == 0:
+            return [pltpu.make_async_copy(weight.at[rows, pl.ds(base, chunk - LANES)],
+                                          wbuf.at[rows, pl.ds(0, chunk - LANES)], ws.at[i, 0])]
+        last = pl.multiple_of(chunks[p - 1] * chunk + chunk - LANES, LANES)
+        return [
+            pltpu.make_async_copy(weight.at[rows, pl.ds(last, LANES)], wbuf.at[rows, pl.ds(0, LANES)], ws.at[i, 0]),
+            pltpu.make_async_copy(weight.at[rows, pl.ds(base, chunk)], wbuf.at[rows, pl.ds(LANES, chunk)], ws.at[i, 1]),
+        ]
+
+    def send(src, dst, send_sem, recv_sem, device):
+        return pltpu.make_async_remote_copy(src_ref=src, dst_ref=dst, send_sem=send_sem, recv_sem=recv_sem,
+                                            device_id=device, device_id_type=MESH)
+
+    def to_plane(k):
+        return send(block(c, z, d), block(c, z, d), s_plane.at[k], ici.at[z, d], (lax.rem(d + k, seqs), v))
+
+    def meta_to(k):
+        return send(meta.at[d], meta.at[d], m_send.at[k], m_recv.at[d], (lax.rem(d + k, seqs), v))
+
+    def to_partner(zc, dc):
+        return send(block(c, zc, dc), block(c, zc, dc), s_part.at[zc, dc], d2d.at[zc, dc], partner)
+
+    def to_above(zc, dc):
+        return send(block(c, zc, dc), block(c, zc, dc), s_right.at[zc, dc], ici.at[zc, dc], above)
+
+    def to_below(zc, dc):
+        return send(block(c, zc, dc), block(c, zc, dc), s_left.at[zc, dc], ici.at[zc, dc], below)
+
+    def from_ici(zc, dc):
+        return send(block(c, zc, dc), block(c, zc, dc), s_part.at[zc, dc], ici.at[zc, dc], partner)
+
+    def from_partner(zc, dc):
+        return send(block(1 - c, zc, dc), block(1 - c, zc, dc), s_part.at[zc, dc], d2d.at[zc, dc], partner)
+
+    small = [
+        pltpu.make_async_copy(labels, lab_v, ms.at[0]),
+        pltpu.make_async_copy(mask, mask_v, ms.at[1]),
+        pltpu.make_async_copy(pair, pair_v, ms.at[2]),
+        pltpu.make_async_copy(flag, flag_v, ms.at[3]),
+        pltpu.make_async_copy(ref, ref_v, ms.at[4]),
+    ]
+    own_rows = [
+        pltpu.make_async_copy(hid.at[0], held.at[c, z, pl.ds(pl.multiple_of(d * columns, columns), length)], xs.at[0]),
+        pltpu.make_async_copy(
+            klh.at[0], held.at[c, z, pl.ds(pl.multiple_of(d * columns + length, length), length)], xs.at[1]),
+    ]
+
+    barrier = pltpu.get_barrier_semaphore()
+    for copy in own_rows + small:
+        copy.start()
+    for k in range(1, seqs):
+        pl.semaphore_signal(barrier, inc=1, device_id=(lax.rem(d + k, seqs), v), device_id_type=MESH)
+    pl.semaphore_signal(barrier, inc=1, device_id=partner, device_id_type=MESH)
+
+    @pl.when(has_above)
+    def _():
+        pl.semaphore_signal(barrier, inc=1, device_id=above, device_id_type=MESH)
+
+    @pl.when(has_below)
+    def _():
+        pl.semaphore_signal(barrier, inc=1, device_id=below, device_id_type=MESH)
+
+    def first_weights(i, carry):
+        for copy in weight_copies(0, i):
+            copy.start()
+        return carry
+
+    lax.fori_loop(0, tiles, first_weights, 0)
+    for copy in own_rows + small:
+        copy.wait()
+    meta[d] = jnp.zeros((8, LANES), jnp.int32)
+    meta[d, 0:1, 0:length] = lab_v[...]
+    meta[d, 1:2, 0:length] = mask_v[...]
+    meta[d, 2:3, :] = jnp.broadcast_to(pair_v[...], (1, LANES))
+    meta[d, 3:4, :] = jnp.broadcast_to(flag_v[...], (1, LANES))
+    pl.semaphore_wait(barrier, seqs + has_above.astype(jnp.int32) + has_below.astype(jnp.int32))
+
+    for k in range(1, seqs):
+        to_plane(k).start()
+    to_partner(z, d).start()
+
+    @pl.when(has_above)
+    def _():
+        to_above(z, d).start()
+
+    @pl.when(has_below)
+    def _():
+        to_below(z, d).start()
+
+    for k in (1, 2, 3) if seqs == 4 else range(1, seqs):
+        dk = lax.rem(d + seqs - k, seqs)
+        from_ici(z, dk).wait_recv()
+        to_partner(z, dk).start()
+
+        @pl.when(has_above)
+        def _():
+            to_above(z, dk).start()
+
+        @pl.when(has_below)
+        def _():
+            to_below(z, dk).start()
+
+    for k in range(1, seqs):
+        meta_to(k).start()
+
+    def relay(step):
+        @pl.when(z - step >= 0)
+        def _():
+            for dc in range(seqs):
+                from_ici(z - step, dc).wait_recv()
+                to_partner(z - step, dc).start()
+
+                @pl.when(has_above)
+                def _():
+                    to_above(z - step, dc).start()
+
+        @pl.when(z + step < depth)
+        def _():
+            for dc in range(seqs):
+                from_ici(z + step, dc).wait_recv()
+                to_partner(z + step, dc).start()
+
+                @pl.when(has_below)
+                def _():
+                    to_below(z + step, dc).start()
+
+    def whole_chunk(zc):
+        for dc in range(seqs):
+            from_partner(zc, dc).wait_recv()
+        return jnp.concatenate([held[0, zc], held[1, zc]], axis=1)
+
+    lane = lax.broadcasted_iota(jnp.int32, (1, LANES), 1)
+    first_row = me * vocab_rows
+
+    def spread(row):
+        own = [meta[s, row:row + 1, :] for s in range(seqs)]
+        parts = []
+        for s in range(seqs):
+            which = meta[s, 2:3, :]
+            other = jnp.zeros((1, LANES), jnp.int32)
+            for t in range(seqs):
+                other = jnp.where(which == t, own[t], other)
+            parts.append(jnp.where(lane < length, own[s], pltpu.roll(other, length, 1)))
+        return jnp.concatenate(
+            [jnp.where(lane < columns, parts[s], pltpu.roll(parts[s + 1], columns, 1)) for s in range(0, seqs, 2)],
+            axis=1)
+
+    for p in range(depth):
+        rows = whole_chunk(chunks[p])
+        if p % 2 == 0:
+            xeven[...] = rows
+            deep = chunk - LANES
+            x_ref = xeven
+        else:
+            xodd[:, 0:LANES] = xeven[:, chunk - LANES:chunk]
+            xodd[:, LANES:chunk + LANES] = rows
+            deep = chunk + LANES
+            x_ref = xodd
+        final = p == depth - 1
+        if final:
+            for k in range(1, seqs):
+                dk = lax.rem(d + seqs - k, seqs)
+                send(meta.at[dk], meta.at[dk], m_send.at[k], m_recv.at[dk], partner).wait_recv()
+            targets = spread(0) - first_row
+            sums[...] = jnp.zeros_like(sums)
+            picks[...] = jnp.zeros_like(picks)
+
+        def one_tile(i, carry, p=p, deep=deep, x_ref=x_ref, final=final):
+            at = pl.ds(pl.multiple_of(i * tile, tile), tile)
+            for copy in weight_copies(p, i):
+                copy.wait()
+            product = lax.dot_general(wbuf[at, 0:deep], x_ref[:, 0:deep], (((1,), (1,)), ((), ())),
+                                      preferred_element_type=jnp.float32)
+            if not final:
+                for copy in weight_copies(p + 1, i):
+                    copy.start()
+
+                @pl.when(i == (tiles * 4) // 5)
+                def _():
+                    relay(p + 1)
+
+            if p == 0:
+                acc[at, :] = product
+            elif not final:
+                acc[at, :] = acc[at, :] + product
+            else:
+                logits = acc[at, :] + product
+                row = lax.broadcasted_iota(jnp.int32, (tile, positions), 0) + i * tile
+                hit = jnp.where(row == targets, logits, 0.0)
+                sums[...] += jnp.sum(jnp.exp(logits).reshape(tile // 8, 8, positions), axis=0)
+                picks[...] += jnp.sum(hit.reshape(tile // 8, 8, positions), axis=0)
+            return carry
+
+        lax.fori_loop(0, tiles, one_tile, 0)
+
+    place = lax.broadcasted_iota(jnp.int32, (1, positions), 1)
+    own_cols = columns // groups
+    base = d * columns + v * own_cols
+    own_ref = jnp.zeros((1, positions), jnp.float32)
+    for j in range(own_cols):
+        own_ref = jnp.where(place == base + j, jnp.broadcast_to(ref_v[0:1, j:j + 1], (1, positions)), own_ref)
+    red[me] = jnp.concatenate(
+        [jnp.sum(sums[...], axis=0, keepdims=True), jnp.sum(picks[...], axis=0, keepdims=True) - own_ref], axis=0)
+
+    def share(k):
+        peer = lax.rem(me + k, devices)
+        return send(red.at[me], red.at[me], r_send.at[k], r_recv.at[me], (lax.div(peer, groups), lax.rem(peer, groups)))
+
+    def send_share(k, carry):
+        share(k).start()
+        return carry
+
+    lax.fori_loop(1, devices, send_share, 0)
+    weights_mask = spread(1).astype(jnp.float32)
+
+    for k in range(1, seqs):
+        to_plane(k).wait_send()
+        meta_to(k).wait_send()
+    for zc in range(depth):
+        for dc in range(seqs):
+            to_partner(zc, dc).wait_send()
+
+            @pl.when(has_above & (z >= zc))
+            def _():
+                to_above(zc, dc).wait_send()
+
+            @pl.when(has_below & (z <= zc))
+            def _():
+                to_below(zc, dc).wait_send()
+
+    def take_share(k, carry):
+        peer = lax.rem(me + k, devices)
+        send(red.at[peer], red.at[peer], r_send.at[k], r_recv.at[peer], partner).wait_recv()
+        return carry
+
+    lax.fori_loop(1, devices, take_share, 0)
+    total = jnp.sum(red[...], axis=0)
+    log_partition = jnp.log(total[0:1])
+    differences = weights_mask * (total[1:2] - log_partition)
+    own_logps = (total[1:2] + own_ref) - log_partition
+    row8 = lax.broadcasted_iota(jnp.int32, (own_cols, positions), 0)
+    lane8 = lax.broadcasted_iota(jnp.int32, (own_cols, positions), 1)
+    out[0:own_cols, :] = jnp.broadcast_to(
+        jnp.sum(jnp.where(lane8 == base + row8, own_logps, 0.0), axis=1, keepdims=True), (own_cols, LANES))
+    within = lax.rem(place, columns)
+    kl_total = jnp.sum(jnp.where(within >= length, differences, 0.0), axis=1, keepdims=True)
+    mean_loss = jnp.zeros((1, 1), jnp.float32)
+    own_loss = jnp.zeros((1, 1), jnp.float32)
+    for s in range(seqs):
+        mine = (place >= s * columns) & (place < s * columns + length)
+        logratio = jnp.sum(jnp.where(mine, differences, 0.0), axis=1, keepdims=True)
+        shift = kto_beta * (logratio - kl_total / seqs)
+        wanted = desirable_weight * (1.0 - 1.0 / (1.0 + jnp.exp(-shift)))
+        unwanted = undesirable_weight * (1.0 - 1.0 / (1.0 + jnp.exp(shift)))
+        one = jnp.where(meta[s, 3:4, 0:1] == 1, wanted, unwanted)
+        mean_loss = mean_loss + one
+        own_loss = jnp.where(d == s, one, own_loss)
+    out[own_cols:own_cols + 1, :] = jnp.broadcast_to(own_loss, (1, LANES))
+    out[own_cols + 1:own_cols + 2, :] = jnp.broadcast_to(mean_loss / seqs, (1, LANES))
+
+    def end_share(k, carry):
+        share(k).wait_send()
+        return carry
+
+    lax.fori_loop(1, devices, end_share, 0)
+
+
+def fused(dims, hidden, kl_hidden, head_weight, labels, token_mask, kl_pair, desirable, ref_logps):
+    seqs, groups = dims
+    depth = groups // 2
+    length, width = hidden.shape[1], hidden.shape[2]
+    columns = 2 * length
+    positions = seqs * columns
+    chunk = 2 * width
+    vocab_rows = head_weight.shape[0]
+    tiles = vocab_rows // TILE_ROWS
+    own_cols = columns // groups
+    devices = seqs * groups
+    dma = pltpu.SemaphoreType.DMA
+    result = pl.pallas_call(
+        functools.partial(fused_kernel, dims),
+        name="kto_head",
+        out_shape=jax.ShapeDtypeStruct((own_cols + 8, LANES), jnp.float32),
+        in_specs=[pl.BlockSpec(memory_space=pltpu.HBM)] * 8,
+        out_specs=pl.BlockSpec(memory_space=pltpu.VMEM),
+        scratch_shapes=[
+            pltpu.VMEM((2, depth, positions, width), jnp.bfloat16),
+            pltpu.VMEM((vocab_rows, chunk + LANES), jnp.bfloat16),
+            pltpu.VMEM((vocab_rows, positions), jnp.float32),
+            pltpu.VMEM((positions, chunk), jnp.bfloat16),
+            pltpu.VMEM((positions, chunk + LANES), jnp.bfloat16),
+            pltpu.VMEM((1, length), jnp.int32),
+            pltpu.VMEM((1, length), jnp.int32),
+            pltpu.VMEM((1, 1), jnp.int32),
+            pltpu.VMEM((1, 1), jnp.int32),
+            pltpu.VMEM((1, own_cols), jnp.float32),
+            pltpu.VMEM((seqs, 8, LANES), jnp.int32),
+            pltpu.VMEM((8, positions), jnp.float32),
+            pltpu.VMEM((8, positions), jnp.float32),
+            pltpu.VMEM((devices, 2, positions), jnp.float32),
+            dma((2,)),
+            dma((5,)),
+            dma((tiles, 2)),
+            dma((depth, seqs)),
+            dma((depth, seqs)),
+            dma((seqs,)),
+            dma((depth, seqs)),
+            dma((depth, seqs)),
+            dma((depth, seqs)),
+            dma((seqs,)),
+            dma((seqs,)),
+            dma((devices,)),
+            dma((devices,)),
+        ],
+        compiler_params=pltpu.CompilerParams(
+            collective_id=0, has_side_effects=True, vmem_limit_bytes=60 * 1024 * 1024),
+    )(hidden, kl_hidden, head_weight, labels, token_mask, kl_pair.reshape(1, 1), desirable.reshape(1, 1), ref_logps)
+    return result[0:own_cols, 0].reshape(1, own_cols), result[own_cols, 0:1], result[own_cols + 1, 0]
+
+
+def on_device(dims, *arrays):
+    hidden, head_weight = arrays[0], arrays[2]
+    seqs, groups = dims
+    fits = (
+        hidden.shape[0] == 1
+        and seqs % 2 == 0
+        and groups % 4 == 0
+        and 4 * hidden.shape[1] == LANES
+        and (2 * hidden.shape[2]) % (2 * LANES) == LANES
+        and head_weight.shape[0] % TILE_ROWS == 0
+        and (2 * hidden.shape[1]) % groups == 0
+    )
+    return fused(dims, *arrays) if fits else gathered_by_xla(*arrays)
+
+
 def solution(mesh):
     in_specs = (
         P("dp", None, "vocab"),
@@ -89,5 +473,5 @@
     )
     out_specs = (P("dp", "vocab"), P("dp"), P())
     return jax.shard_map(
-        on_device, mesh=mesh, in_specs=in_specs, out_specs=out_specs, check_vma=False
-    )
+        functools.partial(on_device, tuple(mesh.shape[a] for a in ("dp", "vocab"))), mesh=mesh, in_specs=in_specs, out_specs=out_specs, check_vma=False
+    )

time: 154 us -> 48.2 us (0.31)
  blocking collectives: 84.9 us -> 0 us
  Pallas kernels: 0 us -> 43.4 us
  matrix products: 25.9 us -> 0 us
  local copies, waits for them, and re-layouts: 18.5 us -> 2.58 us
  between operations: 17.8 us -> 1.93 us
  waiting for transfers between devices: 4.07 us -> 0 us
  other arithmetic: 2.34 us -> 0 us
    pallas_call x0 -> x1, Pallas kernels: none -> 43.4 us  [fused(): pl.pallas_call(functools.partial(fused_kernel, dims), name='kto_head', ou...]
    all_gather x3 -> x0, blocking collectives: 38.8 us -> none  [the longest x1 23.7 us: on_device(): whole_rows = lax.all_gather(combined, 'vocab', axis=2, tiled=True)]
    psum x1 -> x0, blocking collectives: 38.7 us -> none  [on_device(): lax.psum((partition, picked, ref_full), ('dp', 'vocab'))]
    dot_general x1 -> x0, matrix products: 25.9 us -> none  [on_device(): lax.dot_general(portion.reshape(number * columns, model_width), head_weig...]
    gather x4 -> x0, local copies, waits for them, and re-layouts: 10.4 us -> none  [the longest x2 9.27 us: label_terms(): picked = jnp.take_along_axis(logits, clipped[:, None], axis=1)[:, 0]]
    unnamed x1 -> x0, blocking collectives: 7.39 us -> none
    all_gather x1 -> x0, waiting for transfers between devices: 4.05 us -> none  [on_device(): portion = lax.all_gather(whole_rows, 'dp', axis=0, tiled=True)]
    all_gather x1 -> x0, local copies, waits for them, and re-layouts: 3.09 us -> none  [on_device(): whole_rows = lax.all_gather(combined, 'vocab', axis=2, tiled=True)]
  transfers between devices with their start and end apart: 1 -> 0, of which waited for: 1 -> 0; matrix products, arithmetic and copies ran while one was open for 3% -> 0% of each run, Pallas kernels for 0% -> 0%
where the time goes in v1:
time: 48.2 us; the launch traced here: 48 us
  Pallas kernels  43.4 us (90%)
  local copies, waits for them, and re-layouts  2.58 us (5%)
  between operations  1.93 us (4%)
    pallas_call x1, Pallas kernels, fused(): pl.pallas_call(functools.partial(fused_kernel, dims), name='kto_head', ou...  43.4 us
    slice x1, local copies, waits for them, and re-layouts, fused(): result[0:own_cols, 0].reshape(1, own_cols)  1.31 us
    slice x1, local copies, waits for them, and re-layouts, fused(): result[own_cols + 1, 0]  1.28 us

profile of v1, /device:TPU:0, one launch (start us, length us, event | category | flops | bytes accessed | tf_op | source)
XLA Modules:
  0.0 48.0 jit_solution(14021942843782998498)
XLA Ops:
  1.9 43.4 %kto_head.1 = f32[16,128]{1,0:T(8,128)} custom-call(bf16[1,32,448]{2,1,0:T(8,128)(2,1)} %hid.1, bf16[1,32,448]{2,1,0:T(8,128)(2,1)} %klh.1, bf16[8000,3584]{1,0:T(8,128)(2,1)} %weight.1, s32[1,32]{1,0:T(1,128)} %labels.1, s32[1,32]{1,0:T(1,128)} %mask.1, s32[1,1]{1,0:T(1,128)} %bitcast.5.pair, s32[1,1]{1,0:T(1,128)} %bitcast.6.flag, f32[1,8]{1,0:T(1,128)} %ref.1), custom_call_target="tpu_custom_call" | custom-call | tf_op jit(solution)/shard_map/kto_head/pallas_call | solution.py:407
  45.4 1.3 %fusion = (f32[1,1]{1,0:T(1,128)}, f32[1,1]{1,0:T(1,128)}) fusion(f32[16,128]{1,0:T(8,128)} %kto_head.1), kind=kLoop, calls=%fused_computation.1 | loop fusion | bytes 16 | tf_op jit(solution)/shard_map/slice | solution.py:445
  46.6 1.3 %slice_reduce_fusion = f32[8]{0:T(128)} fusion(f32[16,128]{1,0:T(8,128)} %kto_head.1), kind=kLoop, calls=%fused_computation | loop fusion | bytes 64 | tf_op jit(solution)/shard_map/slice | solution.py:445
